TPU v7x, 32 devices: a whole 2x2x4 slice. The times are simulated.
32 devices in a mesh: wide: 8 (over z, y), narrow: 4 (over x, core).
Axes of the slice: x: 2, y: 2, z: 4, core: 2. Of those that a mesh axis runs over, the one named last changes fastest.
Arguments:
- values: float32 [512, 16384], P(('wide', 'narrow')), may hold values from -200 to 200, as said below
- cloud_words: int32 [512, 512], P(('wide', 'narrow')), may hold values from -2147483648 to 2147483647, as said below
- history_len: int32 [1], replicated, may hold values from 96 to 256
- monitor_start: int32 [1], replicated, may hold values from 256 to 384
- boundary_table: int32 [512], replicated, may hold values from 500 to 2000
Outputs:
- ratio: float32 [512, 16384], P(('wide', 'narrow'))
- peak_so_far: float32 [512, 16384], P(('wide', 'narrow'))
Inputs may be any that keep to these rules, and one draw needn't show every extreme that they name: `values`: values of an index series, mixed noise and a seasonal cycle of varying scale. `cloud_words`: bit b of word j in the row of date t is 1 when pixel 32 j + b is clear at date t; the first 16 dates are clear for every pixel.
All inputs are finite; a program needn't handle non-finite values.
Results may differ from a plain program's by a relative error of at most 0.0003.
Values sent between devices are 32-bit elements; how exact they have to be, the bound alone decides.
A program may use at most 64 MiB of HBM per device.

v0:
```python
import math

import jax
import jax.numpy as jnp
from jax import lax
from jax.sharding import PartitionSpec as P

PERIOD = 46
HARMONICS = 3
COLS = 8
WINDOW = 64


HIGH = lax.Precision.HIGHEST


def unpack_clear(words):
    shifts = jnp.arange(32, dtype=jnp.int32)
    flags = jnp.bitwise_and(jnp.right_shift(words[:, :, None], shifts[None, None, :]), jnp.int32(1))
    return flags.reshape(words.shape[0], words.shape[1] * 32).astype(jnp.float32)


def harmonic_design(dates):
    day_float = jnp.arange(dates, dtype=jnp.int32).astype(jnp.float32)
    columns = [jnp.ones((dates,), jnp.float32), day_float / dates]
    for harmonic in range(1, HARMONICS + 1):
        phases = 2.0 * math.pi * harmonic / PERIOD * day_float
        columns.append(jnp.cos(phases))
        columns.append(jnp.sin(phases))
    return jnp.stack(columns, axis=1)


def solve_batched(normal_mat, target):
    size_cols = normal_mat.shape[0]
    factor = [[None] * size_cols for row_idx in range(size_cols)]
    for row_idx in range(size_cols):
        for col_idx in range(row_idx + 1):
            summed = normal_mat[row_idx, col_idx]
            for mid_idx in range(col_idx):
                summed = summed - factor[row_idx][mid_idx] * factor[col_idx][mid_idx]
            if row_idx == col_idx:
                factor[row_idx][col_idx] = jnp.sqrt(summed)
            else:
                factor[row_idx][col_idx] = summed / factor[col_idx][col_idx]
    forward = []
    for row_idx in range(size_cols):
        summed = target[row_idx]
        for mid_idx in range(row_idx):
            summed = summed - factor[row_idx][mid_idx] * forward[mid_idx]
        forward.append(summed / factor[row_idx][row_idx])
    solution = [None] * size_cols
    for row_idx in reversed(range(size_cols)):
        summed = forward[row_idx]
        for mid_idx in range(row_idx + 1, size_cols):
            summed = summed - factor[mid_idx][row_idx] * solution[mid_idx]
        solution[row_idx] = summed / factor[row_idx][row_idx]
    return jnp.stack(solution, axis=0)


def fit_statistic(values, clear, history_len, monitor_start, boundary_table):
    dates = values.shape[0]
    day = jnp.arange(dates, dtype=jnp.int32)
    design = harmonic_design(dates)
    in_history = (day < history_len[0]).astype(jnp.float32)[:, None]
    weight = clear * in_history
    outer = (design[:, :, None] * design[:, None, :]).reshape(dates, COLS * COLS)
    normal_mat = jnp.dot(
        outer.T, weight, precision=HIGH, preferred_element_type=jnp.float32
    ).reshape(COLS, COLS, -1)
    target = jnp.dot(design.T, weight * values, precision=HIGH, preferred_element_type=jnp.float32)
    coeffs = solve_batched(normal_mat, target)
    fitted = jnp.dot(design, coeffs, precision=HIGH, preferred_element_type=jnp.float32)
    resid = clear * (values - fitted)
    count = jnp.sum(weight, axis=0)
    squares = jnp.sum(weight * resid * resid, axis=0)
    sigma = jnp.sqrt(squares / (count - COLS) + 1e-06)
    lagged = day[:, None] - day[None, :]
    banded = ((lagged >= 0) & (lagged < WINDOW)).astype(jnp.float32)
    moving = jnp.dot(banded, resid, precision=HIGH, preferred_element_type=jnp.float32)
    scaled = moving / (sigma * jnp.sqrt(count))[None, :]
    bounds = boundary_table.astype(jnp.float32) * 0.001
    watching = (day >= monitor_start[0])[:, None]
    return jnp.where(watching, scaled / bounds[:, None], jnp.float32(0.0))


def per_device(values, cloud_words, history_len, monitor_start, boundary_table):
    arrived = lax.all_to_all(values, ("wide", "narrow"), split_axis=1, concat_axis=0, tiled=True)
    words = lax.all_to_all(cloud_words, ("wide", "narrow"), split_axis=1, concat_axis=0, tiled=True)
    ratio = fit_statistic(arrived, unpack_clear(words), history_len, monitor_start, boundary_table)
    outgoing = jnp.stack([ratio, lax.cummax(jnp.abs(ratio), axis=0)])
    returned = lax.all_to_all(outgoing, ("wide", "narrow"), split_axis=1, concat_axis=2, tiled=True)
    date_ratio = returned[0]
    peak = returned[1]
    return (date_ratio, peak)


def solution(mesh):
    placed = (P(("wide", "narrow"), None), P(("wide", "narrow"), None), P(), P(), P())
    return jax.shard_map(
        per_device,
        mesh=mesh,
        in_specs=placed,
        out_specs=(P(("wide", "narrow"), None), P(("wide", "narrow"), None)),
        check_vma=False,
    )
```

profile of v0, /device:TPU:0, one launch (start us, length us, event | category | flops | bytes accessed | tf_op | source)
XLA Modules:
  0.0 109.6 jit_solution(6393028635520491719)
XLA Ops:
  0.6 0.9 all_to_all.37
  1.7 0.8 reshape.2545
  2.4 7.3 %all-to-all-start = ((s32[32,1,256]{2,1,0:T(1,128)}), s32[32,1,256]{2,1,0:T(1,128)S(1)}, u32[]{:S(2)}, u32[]{:S(2)}) async-start(s32[32,1,256]{2,1,0:T(1,128)} %reshape.2545), calls=%async_computation | async-start | bytes 65536 | tf_op jit(solution)/shard_map/all_to_all | solution.py:88
  11.3 2.3 %copy.58 = f32[2,32,8,512]{3,2,0,1:T(8,128)} copy(f32[2,32,8,512]{3,2,1,0:T(8,128)} %bitcast.465) | data formatting | bytes 2097152 | tf_op jit(solution)/shard_map/all_to_all | solution.py:87
  13.7 3.3 %all-to-all-done = s32[32,1,256]{2,1,0:T(1,128)S(1)} async-done(((s32[32,1,256]{2,1,0:T(1,128)}), s32[32,1,256]{2,1,0:T(1,128)S(1)}, u32[]{:S(2)}, u32[]{:S(2)}) %all-to-all-start) | async-done | bytes 32800 | tf_op jit(solution)/shard_map/all_to_all | solution.py:88
  17.0 2.6 %all-to-all-start.1 = ((f32[16,32,512]{2,0,1:T(8,128)}), f32[16,32,512]{2,0,1:T(8,128)S(1)}, u32[]{:S(2)}, u32[]{:S(2)}) async-start(f32[16,32,512]{2,0,1:T(8,128)} %bitcast.446), calls=%async_computation.1 | async-start | bytes 2097152 | tf_op jit(solution)/shard_map/all_to_all | solution.py:87
  19.9 0.5 broadcast.145
  20.5 0.7 reduce.1
  21.5 0.3 copy.33
  22.3 1.1 %fusion.15 = f32[8,8,512]{2,1,0:T(8,128)S(1)} fusion(f32[512,512,1]{0,1,2:T(8,128)S(1)} %bitcast.457, f32[512,8]{0,1:T(8,128)S(1)} %stack.10), kind=kOutput, calls=%fused_computation.26 | convolution fusion | flops 201359360 | bytes 1196032 | tf_op jit(solution)/shard_map/dot_general | solution.py:67
  23.6 22.3 %all-to-all-done.1 = f32[16,32,512]{2,0,1:T(8,128)S(1)} async-done(((f32[16,32,512]{2,0,1:T(8,128)}), f32[16,32,512]{2,0,1:T(8,128)S(1)}, u32[]{:S(2)}, u32[]{:S(2)}) %all-to-all-start.1) | async-done | bytes 1048608 | tf_op jit(solution)/shard_map/all_to_all | solution.py:87
  46.1 0.6 fusion.126
  47.2 1.3 %fusion.1 = (f32[512]{0:T(512)S(1)}, f32[512,512]{1,0:T(8,128)S(1)}) fusion(s32[512,512]{1,0:T(8,128)S(1)} %copy.33, f32[512]{0:T(512)S(1)} %fusion.100, s32[512]{0:T(512)S(1)} %shift_right_arithmetic.38, f32[512,512]{1,0:T(8,128)S(1)} %bitcast.453, f32[512,8]{0,1:T(8,128)S(1)} %stack.10, f32[8,512]{1,0:T(8,128)S(1)} %stack.11), kind=kOutput, calls=%fused_computation.4 | convolution fusion | flops 27524608 | bytes 3184640 | tf_op jit(solution)/shard_map/dot_general | solution.py:72
  48.5 1.1 fusion.9
  49.6 0.3 copy.36
  49.9 0.4 select_bitcast_fusion
  50.4 0.7 fusion.4
  51.2 0.6 copy.38
  52.1 2.4 %copy.39 = f32[2,512,512]{2,0,1:T(2,128)} copy(f32[2,512,512]{1,2,0:T(8,128)S(1)} %pad_maximum_fusion) | data formatting | bytes 4194304 | tf_op jit(solution)/shard_map/stack | solution.py:90
  54.5 52.2 %all_to_all.50 = f32[2,512,512]{2,0,1:T(2,128)S(1)} all-to-all(f32[2,512,512]{2,0,1:T(2,128)} %copy.39), channel_id=1, replica_groups=mesh['wide'=8,'narrow'=4] {'wide','narrow'}, dimensions={1} | all-to-all | bytes 4194304 | tf_op jit(solution)/shard_map/all_to_all | solution.py:91
  106.8 0.4 copy.40
  107.2 0.3 fusion.125
  107.5 1.1 copy.49
  108.5 1.0 copy.48
  (37 shorter events, 2.7 us)
Async XLA Ops:
  2.4 14.6 %all-to-all-start = ((s32[32,1,256]{2,1,0:T(1,128)}), s32[32,1,256]{2,1,0:T(1,128)S(1)}, u32[]{:S(2)}, u32[]{:S(2)}) async-start(s32[32,1,256]{2,1,0:T(1,128)} %reshape.2545), calls=%async_computation | async-start | bytes 65536 | tf_op jit(solution)/shard_map/all_to_all | solution.py:88
  11.3 8.6 %copy-start = (s32[512]{0:T(512)S(1)}, s32[512]{0:T(512)}, u32[]{:S(2)}) copy-start(s32[512]{0:T(512)} %param.9) | copy-start | bytes 6148
  17.0 28.8 %all-to-all-start.1 = ((f32[16,32,512]{2,0,1:T(8,128)}), f32[16,32,512]{2,0,1:T(8,128)S(1)}, u32[]{:S(2)}, u32[]{:S(2)}) async-start(f32[16,32,512]{2,0,1:T(8,128)} %bitcast.446), calls=%async_computation.1 | async-start | bytes 2097152 | tf_op jit(solution)/shard_map/all_to_all | solution.py:87
where the time goes:
time: 110 us
  blocking collectives  52.2 us (47%)
  waiting for transfers between devices  25.6 us (23%)
  local copies, waits for them, and re-layouts  11.9 us (11%)
  starting transfers between devices  9.97 us (9%)
  matrix products  4.08 us (4%)
  other arithmetic  3.62 us (3%)
  between operations  2.2 us (2%)
    all_to_all x1, blocking collectives, per_device(): lax.all_to_all(outgoing, ('wide', 'narrow'), split_axis=1, concat_axis=2,...  52.2 us
    all_to_all x1, waiting for transfers between devices, per_device(): lax.all_to_all(values, ('wide', 'narrow'), split_axis=1, concat_axis=0, t...  22.3 us
    all_to_all x1, starting transfers between devices, per_device(): lax.all_to_all(cloud_words, ('wide', 'narrow'), split_axis=1, concat_axis...  7.33 us
    all_to_all x1, waiting for transfers between devices, per_device(): lax.all_to_all(cloud_words, ('wide', 'narrow'), split_axis=1, concat_axis...  3.31 us
    unnamed x8, local copies, waits for them, and re-layouts  3.07 us
    another operation x2, local copies, waits for them, and re-layouts, per_device(): outgoing = jnp.stack([ratio, lax.cummax(jnp.abs(ratio), axis=0)])  3.02 us
    all_to_all x1, starting transfers between devices, per_device(): lax.all_to_all(values, ('wide', 'narrow'), split_axis=1, concat_axis=0, t...  2.65 us
    all_to_all x1, local copies, waits for them, and re-layouts, per_device(): lax.all_to_all(values, ('wide', 'narrow'), split_axis=1, concat_axis=0, t...  2.3 us
  transfers between devices with their start and end apart: 2, of which 2 were waited for; matrix products, arithmetic and copies ran while one was open for 6% of the time, Pallas kernels for 0%

commit v1 on v0

--- a/solution.py
+++ b/solution.py
@@ -87,10 +87,13 @@
     arrived = lax.all_to_all(values, ("wide", "narrow"), split_axis=1, concat_axis=0, tiled=True)
     words = lax.all_to_all(cloud_words, ("wide", "narrow"), split_axis=1, concat_axis=0, tiled=True)
     ratio = fit_statistic(arrived, unpack_clear(words), history_len, monitor_start, boundary_table)
-    outgoing = jnp.stack([ratio, lax.cummax(jnp.abs(ratio), axis=0)])
-    returned = lax.all_to_all(outgoing, ("wide", "narrow"), split_axis=1, concat_axis=2, tiled=True)
-    date_ratio = returned[0]
-    peak = returned[1]
+    rows = values.shape[0]
+    blocks = ratio.reshape(ratio.shape[0] // rows, rows, ratio.shape[1])
+    block_peak = lax.cummax(jnp.max(jnp.abs(blocks), axis=1), axis=0)
+    earlier = jnp.concatenate([jnp.zeros_like(block_peak[:1]), block_peak[:-1]], axis=0)
+    date_ratio = lax.all_to_all(ratio, ("wide", "narrow"), split_axis=0, concat_axis=1, tiled=True)
+    before = lax.all_to_all(earlier, ("wide", "narrow"), split_axis=0, concat_axis=1, tiled=True)
+    peak = jnp.maximum(lax.cummax(jnp.abs(date_ratio), axis=0), before)
     return (date_ratio, peak)
 
 

time: 110 us -> 93.1 us (0.85)
  blocking collectives: 52.2 us -> 0 us
  waiting for transfers between devices: 25.6 us -> 57 us
  starting transfers between devices: 9.97 us -> 17.1 us
  local copies, waits for them, and re-layouts: 11.9 us -> 6.78 us
  matrix products: 4.08 us -> 5.22 us
    all_to_all x1 -> x0, blocking collectives: 52.2 us -> none  [per_device(): lax.all_to_all(outgoing, ('wide', 'narrow'), split_axis=1, concat_axis=2,...]
    all_to_all x0 -> x2, waiting for transfers between devices: none -> 30.8 us  [the longest x1 25.4 us: per_device(): lax.all_to_all(ratio, ('wide', 'narrow'), split_axis=0, concat_axis=1, ti...]
    all_to_all x0 -> x2, starting transfers between devices: none -> 7.16 us  [the longest x1 3.62 us: per_device(): lax.all_to_all(earlier, ('wide', 'narrow'), split_axis=0, concat_axis=1,...]
    another operation x4 -> x0, local copies, waits for them, and re-layouts: 3.03 us -> none  [the longest x2 3.02 us: per_device(): outgoing = jnp.stack([ratio, lax.cummax(jnp.abs(ratio), axis=0)])]
    all_to_all x1, local copies, waits for them, and re-layouts: 2.3 us -> 1.06 us  [per_device(): lax.all_to_all(values, ('wide', 'narrow'), split_axis=1, concat_axis=0, t...]
    all_to_all x1, waiting for transfers between devices: 3.31 us -> 4.54 us  [per_device(): lax.all_to_all(cloud_words, ('wide', 'narrow'), split_axis=1, concat_axis...]
    dot_general x1, matrix products: 1.08 us -> 2.22 us  [fit_statistic(): jnp.dot(banded, resid, precision=HIGH, preferred_element_type=jnp.float32)]
  transfers between devices with their start and end apart: 2 -> 4, of which waited for: 2 -> 4; matrix products, arithmetic and copies ran while one was open for 6% -> 8% of each run, Pallas kernels for 0% -> 0%
where the time goes in v1:
time: 93.1 us; the launch traced here: 92.7 us
  waiting for transfers between devices  57 us (61%)
  starting transfers between devices  17.1 us (18%)
  local copies, waits for them, and re-layouts  6.78 us (7%)
  matrix products  5.22 us (6%)
  other arithmetic  4.33 us (5%)
  between operations  2.16 us (2%)
    all_to_all x1, waiting for transfers between devices, per_device(): lax.all_to_all(ratio, ('wide', 'narrow'), split_axis=0, concat_axis=1, ti...  25.4 us
    all_to_all x1, waiting for transfers between devices, per_device(): lax.all_to_all(values, ('wide', 'narrow'), split_axis=1, concat_axis=0, t...  21.7 us
    all_to_all x1, starting transfers between devices, per_device(): lax.all_to_all(cloud_words, ('wide', 'narrow'), split_axis=1, concat_axis...  7.33 us
    all_to_all x1, waiting for transfers between devices, per_device(): lax.all_to_all(earlier, ('wide', 'narrow'), split_axis=0, concat_axis=1,...  5.43 us
    all_to_all x1, waiting for transfers between devices, per_device(): lax.all_to_all(cloud_words, ('wide', 'narrow'), split_axis=1, concat_axis...  4.54 us
    all_to_all x1, starting transfers between devices, per_device(): lax.all_to_all(earlier, ('wide', 'narrow'), split_axis=0, concat_axis=1,...  3.62 us
    all_to_all x1, starting transfers between devices, per_device(): lax.all_to_all(ratio, ('wide', 'narrow'), split_axis=0, concat_axis=1, ti...  3.54 us
    all_to_all x1, starting transfers between devices, per_device(): lax.all_to_all(values, ('wide', 'narrow'), split_axis=1, concat_axis=0, t...  2.65 us
  transfers between devices with their start and end apart: 4, of which 4 were waited for; matrix products, arithmetic and copies ran while one was open for 8% of the time, Pallas kernels for 0%

profile of v1, /device:TPU:0, one launch (start us, length us, event | category | flops | bytes accessed | tf_op | source)
XLA Modules:
  0.0 92.7 jit_solution(12139132134094349845)
XLA Ops:
  0.6 1.0 %all_to_all.50 = s32[16,32,16]{2,1,0:T(8,128)S(1)} reshape(s32[16,512]{1,0:T(8,128)} %param.6) | data formatting | bytes 65536 | tf_op jit(solution)/shard_map/all_to_all | solution.py:88
  1.8 0.8 reshape.2540
  2.5 7.3 %all-to-all-start = ((s32[32,1,256]{2,1,0:T(1,128)}), s32[32,1,256]{2,1,0:T(1,128)S(1)}, u32[]{:S(2)}, u32[]{:S(2)}) async-start(s32[32,1,256]{2,1,0:T(1,128)} %reshape.2540), calls=%async_computation | async-start | bytes 65536 | tf_op jit(solution)/shard_map/all_to_all | solution.py:88
  11.4 1.1 %copy.28 = f32[2,32,8,512]{3,2,0,1:T(8,128)} copy(f32[2,32,8,512]{3,2,1,0:T(8,128)S(1)} %bitcast.435) | data formatting | bytes 2097152 | tf_op jit(solution)/shard_map/all_to_all | solution.py:87
  12.6 4.5 %all-to-all-done = s32[32,1,256]{2,1,0:T(1,128)S(1)} async-done(((s32[32,1,256]{2,1,0:T(1,128)}), s32[32,1,256]{2,1,0:T(1,128)S(1)}, u32[]{:S(2)}, u32[]{:S(2)}) %all-to-all-start) | async-done | bytes 32800 | tf_op jit(solution)/shard_map/all_to_all | solution.py:88
  17.1 2.6 %all-to-all-start.1 = ((f32[16,32,512]{2,0,1:T(8,128)}), f32[16,32,512]{2,0,1:T(8,128)S(1)}, u32[]{:S(2)}, u32[]{:S(2)}) async-start(f32[16,32,512]{2,0,1:T(8,128)} %bitcast.423), calls=%async_computation.1 | async-start | bytes 2097152 | tf_op jit(solution)/shard_map/all_to_all | solution.py:87
  20.0 0.7 copy-done.2
  20.7 0.5 broadcast.136
  21.2 0.7 reduce.1
  22.3 0.3 copy.16
  22.6 0.3 fusion.10
  23.1 1.1 %fusion.11 = f32[8,8,512]{2,1,0:T(8,128)S(1)} fusion(f32[512,512,1]{0,1,2:T(8,128)S(1)} %bitcast.432, f32[512,8]{0,1:T(8,128)S(1)} %stack.4), kind=kOutput, calls=%fused_computation.20 | convolution fusion | flops 201359360 | bytes 1196032 | tf_op jit(solution)/shard_map/dot_general | solution.py:67
  24.3 21.7 %all-to-all-done.1 = f32[16,32,512]{2,0,1:T(8,128)S(1)} async-done(((f32[16,32,512]{2,0,1:T(8,128)}), f32[16,32,512]{2,0,1:T(8,128)S(1)}, u32[]{:S(2)}, u32[]{:S(2)}) %all-to-all-start.1) | async-done | bytes 1048608 | tf_op jit(solution)/shard_map/all_to_all | solution.py:87
  46.2 0.6 fusion.121
  47.3 1.3 %fusion.2 = (f32[512]{0:T(512)S(1)}, f32[512,512]{1,0:T(8,128)S(1)}) fusion(s32[512,512]{1,0:T(8,128)S(1)} %copy.16, f32[512]{0:T(512)S(1)} %fusion.96, s32[512]{0:T(512)S(1)} %shift_right_arithmetic.38, f32[512,512]{1,0:T(8,128)S(1)} %bitcast.428, f32[512,8]{0,1:T(8,128)S(1)} %stack.4, f32[8,512]{1,0:T(8,128)S(1)} %stack.5), kind=kOutput, calls=%fused_computation.5 | convolution fusion | flops 27524608 | bytes 3184640 | tf_op jit(solution)/shard_map/dot_general | solution.py:72
  48.6 2.2 %abs_reduce_fusion = (f32[32,512]{1,0:T(8,128)S(1)}, f32[512,512]{1,0:T(8,128)}) fusion(f32[512]{0:T(512)S(1)} %convert_multiply_fusion.2, f32[512]{0:T(512)S(1)} %sqrt_multiply_fusion, f32[512,512]{1,0:T(8,128)S(1)} %get-tuple-element.85, pred[512]{0:T(512)(128)(4,1)S(1)} %iota_compare_fusion.1), kind=kOutput, calls=%fused_computation.8 | convolution fusion | flops 1612955648 | bytes 2167296 | tf_op jit(solution)/shard_map/dot_general | solution.py:79
  50.8 3.5 %all-to-all-start.2 = ((f32[32,16,512]{2,1,0:T(8,128)}), f32[32,16,512]{2,1,0:T(8,128)S(1)}, u32[]{:S(2)}, u32[]{:S(2)}) async-start(f32[32,16,512]{2,1,0:T(8,128)} %bitcast.50), calls=%async_computation.2 | async-start | bytes 2097152 | tf_op jit(solution)/shard_map/all_to_all | solution.py:94
  54.5 0.7 copy.20
  55.2 25.4 %all-to-all-done.2 = f32[32,16,512]{2,1,0:T(8,128)S(1)} async-done(((f32[32,16,512]{2,1,0:T(8,128)}), f32[32,16,512]{2,1,0:T(8,128)S(1)}, u32[]{:S(2)}, u32[]{:S(2)}) %all-to-all-start.2) | async-done | bytes 1048608 | tf_op jit(solution)/shard_map/all_to_all | solution.py:94
  80.6 3.6 %all-to-all-start.3 = ((f32[32,1,512]{2,1,0:T(1,128)}), f32[32,1,512]{2,1,0:T(1,128)S(1)}, u32[]{:S(2)}, u32[]{:S(2)}) async-start(f32[32,1,512]{2,1,0:T(1,128)} %copy.20), calls=%async_computation.3 | async-start | bytes 131072 | tf_op jit(solution)/shard_map/all_to_all | solution.py:95
  84.4 0.9 copy-done
  85.3 0.9 reduce_window_max.20
  86.2 5.4 %all-to-all-done.3 = f32[32,1,512]{2,1,0:T(1,128)S(1)} async-done(((f32[32,1,512]{2,1,0:T(1,128)}), f32[32,1,512]{2,1,0:T(1,128)S(1)}, u32[]{:S(2)}, u32[]{:S(2)}) %all-to-all-start.3) | async-done | bytes 65568 | tf_op jit(solution)/shard_map/all_to_all | solution.py:95
  91.6 1.1 %broadcast_maximum_fusion = f32[16,16384]{1,0:T(8,128)} fusion(f32[16,16384]{1,0:T(8,128)S(1)} %reduce_window_max.20, f32[16384]{0:T(1024)S(1)} %bitcast.437), kind=kLoop, calls=%fused_computation.16 | loop fusion | flops 262144 | bytes 2162688 | tf_op jit(solution)/shard_map/max | solution.py:96
  (35 shorter events, 2.3 us)
Async XLA Ops:
  0.6 10.8 %copy-start.1 = (f32[16,16384]{1,0:T(8,128)S(1)}, f32[16,16384]{1,0:T(8,128)}, u32[]{:S(2)}) copy-start(f32[16,16384]{1,0:T(8,128)} %param.5) | copy-start | bytes 3145732
  2.5 14.6 %all-to-all-start = ((s32[32,1,256]{2,1,0:T(1,128)}), s32[32,1,256]{2,1,0:T(1,128)S(1)}, u32[]{:S(2)}, u32[]{:S(2)}) async-start(s32[32,1,256]{2,1,0:T(1,128)} %reshape.2540), calls=%async_computation | async-start | bytes 65536 | tf_op jit(solution)/shard_map/all_to_all | solution.py:88
  17.1 28.8 %all-to-all-start.1 = ((f32[16,32,512]{2,0,1:T(8,128)}), f32[16,32,512]{2,0,1:T(8,128)S(1)}, u32[]{:S(2)}, u32[]{:S(2)}) async-start(f32[16,32,512]{2,0,1:T(8,128)} %bitcast.423), calls=%async_computation.1 | async-start | bytes 2097152 | tf_op jit(solution)/shard_map/all_to_all | solution.py:87
  20.0 0.7 copy-start.2
  50.8 29.8 %all-to-all-start.2 = ((f32[32,16,512]{2,1,0:T(8,128)}), f32[32,16,512]{2,1,0:T(8,128)S(1)}, u32[]{:S(2)}, u32[]{:S(2)}) async-start(f32[32,16,512]{2,1,0:T(8,128)} %bitcast.50), calls=%async_computation.2 | async-start | bytes 2097152 | tf_op jit(solution)/shard_map/all_to_all | solution.py:94
  80.6 11.0 %all-to-all-start.3 = ((f32[32,1,512]{2,1,0:T(1,128)}), f32[32,1,512]{2,1,0:T(1,128)S(1)}, u32[]{:S(2)}, u32[]{:S(2)}) async-start(f32[32,1,512]{2,1,0:T(1,128)} %copy.20), calls=%async_computation.3 | async-start | bytes 131072 | tf_op jit(solution)/shard_map/all_to_all | solution.py:95
  84.3 1.0 %copy-start = (f32[32,2,8,512]{3,2,0,1:T(8,128)}, f32[32,2,8,512]{3,2,0,1:T(8,128)S(1)}, u32[]{:S(2)}) copy-start(f32[32,2,8,512]{3,2,0,1:T(8,128)S(1)} %copy.25) | copy-start | bytes 3145732

commit v2 on v1

--- a/solution.py
+++ b/solution.py
@@ -1,8 +1,12 @@
+import functools
 import math
 
 import jax
 import jax.numpy as jnp
 from jax import lax
+from jax.experimental import pallas as pl
+from jax.experimental.pallas import tpu as pltpu
+import numpy as np
 from jax.sharding import PartitionSpec as P
 
 PERIOD = 46
@@ -97,10 +101,488 @@
     return (date_ratio, peak)
 
 
+HISTORY_MOST = 256
+MESH = pl.DeviceIdType.MESH
+
+
+def host_design(dates):
+    day = np.arange(dates, dtype=np.float32)
+    columns = [np.ones((dates,), np.float32), (day / np.float32(dates)).astype(np.float32)]
+    for harmonic in range(1, HARMONICS + 1):
+        phases = (np.float32(2.0 * math.pi * harmonic / PERIOD) * day).astype(np.float64)
+        columns.append(np.cos(phases).astype(np.float32))
+        columns.append(np.sin(phases).astype(np.float32))
+    return np.stack(columns, axis=1)
+
+
+def dot_high(left, right):
+    return jnp.dot(left, right, precision=HIGH, preferred_element_type=jnp.float32)
+
+
+def clear_bits(words, offset, pixels):
+    rows, lanes = words.shape
+    parts = [((words >> (8 * k)) & 255).astype(jnp.float32).astype(jnp.bfloat16) for k in range(4)]
+    stacked = jnp.concatenate(parts, axis=0)
+    word_of = lax.broadcasted_iota(jnp.int32, (lanes, pixels), 1) >> 5
+    spread = (lax.broadcasted_iota(jnp.int32, (lanes, pixels), 0) - offset == word_of)
+    spread = spread.astype(jnp.float32).astype(jnp.bfloat16)
+    wide = jnp.dot(stacked, spread, preferred_element_type=jnp.float32)
+    lane = lax.broadcasted_iota(jnp.int32, (rows, pixels), 1)
+    which = (lane >> 3) & 3
+    byte = wide[:rows]
+    for k in range(1, 4):
+        byte = jnp.where(which == k, wide[k * rows : (k + 1) * rows], byte)
+    return ((byte.astype(jnp.int32) >> (lane & 7)) & 1).astype(jnp.float32)
+
+
+def scan_rows(array, combine, neutral):
+    rows = array.shape[0]
+    row = lax.broadcasted_iota(jnp.int32, array.shape, 0)
+    step = 1
+    while step < rows:
+        shifted = jnp.where(row >= step, pltpu.roll(array, step, 0), neutral)
+        array = combine(array, shifted)
+        step *= 2
+    return array
+
+
+def solve_rows(entry, target):
+    factor = [[None] * COLS for _ in range(COLS)]
+    inverse = [None] * COLS
+    for i in range(COLS):
+        for j in range(i + 1):
+            summed = entry(i, j)
+            for m in range(j):
+                summed = summed - factor[i][m] * factor[j][m]
+            if i == j:
+                inverse[i] = 1.0 / jnp.sqrt(summed)
+            else:
+                factor[i][j] = summed * inverse[j]
+    forward = []
+    for i in range(COLS):
+        summed = target(i)
+        for m in range(i):
+            summed = summed - factor[i][m] * forward[m]
+        forward.append(summed * inverse[i])
+    answer = [None] * COLS
+    for i in reversed(range(COLS)):
+        summed = forward[i]
+        for m in range(i + 1, COLS):
+            summed = summed - factor[m][i] * answer[m]
+        answer[i] = summed * inverse[i]
+    return answer
+
+
+def fused_kernel(
+    narrow, chips, hist, back,
+    hl_ref, ms_ref, v_ref, w_ref, d_ref, dt_ref, ot_ref, b_ref, ratio_ref, peak_ref,
+    cv, cw, ccl, hv, hw, ow, tp, tb, nm, cb, cnt, sq, sb, tot, tt, sc, scb, rt, mrow, mb,
+    ax_s, ax_r, ha_s, ha_r, hw_s, hw_r, ow_s, ow_r, tp_s, tp_r, cb_s, cb_r, ct_s, ct_r,
+    sq_s, sq_r, tt_s, tt_r, sc_s, sc_r, mx_s, mx_r, or_s, or_r, op_s, op_r, lc,
+):
+    me = lax.axis_index("wide") * narrow + lax.axis_index("narrow")
+    q, c = lax.div(me, 2), lax.rem(me, 2)
+    rows, pixels = v_ref.shape
+    half = pixels // 2
+    own = half // hist
+    slots = hist
+    chip_rows = 2 * rows
+    late = chips - hist
+    is_hist = q < hist
+    is_late = q >= hist
+
+    def dev(q2, c2):
+        d = 2 * q2 + c2
+        return (lax.div(d, narrow), lax.rem(d, narrow))
+
+    def remote(src, dst, ssem, rsem, q2, c2):
+        return pltpu.make_async_remote_copy(
+            src_ref=src, dst_ref=dst, send_sem=ssem, recv_sem=rsem,
+            device_id=dev(q2, c2), device_id_type=MESH)
+
+    def cols(s):
+        return pl.ds(pl.multiple_of(s * own, own), own)
+
+    mine = pl.ds(pl.multiple_of(c * rows, rows), rows)
+    theirs = pl.ds(pl.multiple_of((1 - c) * rows, rows), rows)
+    my_half = pl.ds(pl.multiple_of(c * half, half), half)
+    other_half = pl.ds(pl.multiple_of((1 - c) * half, half), half)
+
+    def half_col(h, s):
+        return pl.ds(pl.multiple_of(h * half + s * own, own), own)
+
+    swap_v = remote(v_ref.at[:, other_half], cv.at[mine, :], ax_s.at[0], ax_r.at[0], q, 1 - c)
+    swap_w = remote(w_ref, cw.at[mine, :], ax_s.at[1], ax_r.at[1], q, 1 - c)
+    swap_w.start()
+    swap_v.start()
+    keep_v = pltpu.make_async_copy(v_ref.at[:, my_half], cv.at[mine, :], lc.at[0])
+    keep_w = pltpu.make_async_copy(w_ref, cw.at[mine, :], lc.at[1])
+    keep_v.start()
+    keep_w.start()
+
+    def owner_block(q2, c2):
+        return pl.ds(pl.multiple_of(lax.div(c2 * half + q2 * own, 32 * 128) * 128, 128), 128)
+
+    my_dates = pl.ds(pl.multiple_of(me * rows, rows), rows)
+    keep_o = pltpu.make_async_copy(w_ref.at[:, owner_block(q, c)], ow.at[my_dates, :], lc.at[2])
+
+    def send_words(k):
+        to = lax.rem(me + k, 2 * hist)
+        return remote(w_ref.at[:, owner_block(lax.div(to, 2), lax.rem(to, 2))],
+                      ow.at[my_dates, :], ow_s.at[k - 1], ow_r.at[k - 1],
+                      lax.div(to, 2), lax.rem(to, 2))
+
+    @pl.when(is_hist)
+    def _():
+        @pl.loop(1, 2 * hist)
+        def _(k):
+            send_words(k).start()
+        keep_o.start()
+
+    sends_early = jnp.logical_and(q + back >= hist, q + back < chips)
+
+    def early_words(h):
+        return remote(w_ref, hw.at[mine, :], hw_s.at[h], hw_r.at[c], q + back, h)
+
+    def early(h, s):
+        return remote(v_ref.at[:, half_col(h, s)], hv.at[mine, cols(s)],
+                      ha_s.at[h * slots + s], ha_r.at[c * slots + s], q + back, h)
+
+    @pl.when(sends_early)
+    def _():
+        for h in range(2):
+            early_words(h).start()
+
+        @pl.loop(0, slots)
+        def _(s):
+            early(0, s).start()
+            early(1, s).start()
+
+    def word_block(s):
+        start = c * (half // 32) + s * (own // 32)
+        base = lax.div(start, 128) * 128
+        return pl.ds(pl.multiple_of(base, 128), 128), start - base
+
+    keep_w.wait()
+    swap_w.wait_recv()
+
+    @pl.loop(0, slots)
+    def _(s):
+        block, offset = word_block(s)
+        ccl[:, cols(s)] = clear_bits(cw[:, block], offset, own)
+
+    keep_v.wait()
+    swap_v.wait_recv()
+    date = q * chip_rows + lax.broadcasted_iota(jnp.int32, (chip_rows, own), 0)
+
+    def send_target(k):
+        to = lax.rem(q + k, hist)
+        return remote(tp.at[to], tb.at[q], tp_s.at[k - 1], tp_r.at[k - 1], to, c)
+
+    def send_coeffs(k, base):
+        return remote(cb.at[q - base], cb.at[q - base], cb_s.at[k - 1], cb_r.at[k - 1],
+                      base + lax.rem(q - base + k, hist), c)
+
+    relay = remote(cb.at[q], cb.at[q], cb_s.at[hist - 1], cb_r.at[hist - 1], q + hist, c)
+    give_count = remote(cnt, cnt, ct_s.at[0], ct_r.at[0], q + hist, c)
+
+    @pl.when(is_hist)
+    def _():
+        @pl.loop(0, slots)
+        def _(s):
+            weighted = jnp.where(date < hl_ref[0], ccl[:, cols(s)] * cv[:, cols(s)], 0.0)
+            tp[s] = dot_high(dt_ref[q], weighted)
+
+        @pl.loop(1, hist)
+        def _(k):
+            send_target(k).start()
+
+        ratio_ref[...] = jnp.zeros_like(ratio_ref)
+        peak_ref[...] = jnp.zeros_like(peak_ref)
+        keep_o.wait()
+
+        @pl.loop(1, 2 * hist)
+        def _(k):
+            send_words(k).wait_recv()
+
+        start = c * (half // 32) + q * (own // 32)
+        flags = clear_bits(ow[...], lax.rem(start, 128), own)
+        day = lax.broadcasted_iota(jnp.int32, flags.shape, 0)
+        nm[...] = dot_high(ot_ref[...], jnp.where(day < hl_ref[0], flags, 0.0))
+        cnt[...] = nm[0:1, :]
+        give_count.start()
+        total = tp[q]
+
+        @pl.loop(1, hist)
+        def _(k):
+            send_target(k).wait_recv()
+
+        tb[q] = total
+        total = tb[0]
+        for s in range(1, hist):
+            total = total + tb[s]
+        tb[q] = total
+
+        def entry(i, j):
+            at = i * (i + 1) // 2 + j
+            return nm[at : at + 1, :]
+
+        answer = solve_rows(entry, lambda i: tb[q, i : i + 1, :])
+        for i in range(COLS):
+            cb[q, i : i + 1, :] = answer[i]
+        relay.start()
+
+        @pl.loop(1, hist)
+        def _(k):
+            send_coeffs(k, 0).start()
+
+        @pl.loop(1, hist)
+        def _(k):
+            send_coeffs(k, 0).wait_recv()
+
+    @pl.when(is_late)
+    def _():
+        for h in range(2):
+            remote(w_ref, hw.at[pl.ds(h * rows, rows), :], hw_s.at[h], hw_r.at[h], q, 1 - c).wait_recv()
+        remote(cb.at[q - hist], cb.at[q - hist], cb_s.at[hist - 1], cb_r.at[hist - 1], q - hist, c).wait_recv()
+
+        @pl.loop(1, hist)
+        def _(k):
+            send_coeffs(k, hist).start()
+
+        @pl.loop(1, hist)
+        def _(k):
+            send_coeffs(k, hist).wait_recv()
+
+    @pl.loop(0, slots)
+    def _(s):
+        resid = ccl[:, cols(s)] * (cv[:, cols(s)] - dot_high(d_ref[q], cb[s]))
+        cv[:, cols(s)] = resid
+        tot[0:1, cols(s)] = jnp.sum(resid, axis=0, keepdims=True)
+        sq[s] = jnp.sum(jnp.where(date < hl_ref[0], resid * resid, 0.0), axis=0, keepdims=True)
+
+    def send_total(j):
+        return remote(tot, tt.at[j - 1], tt_s.at[j - 1], tt_r.at[j - 1], q + j, c)
+
+    for j in range(1, back):
+        @pl.when(jnp.logical_and(q + j >= hist, q + j < chips))
+        def _():
+            send_total(j).start()
+
+    def send_squares(s):
+        return remote(sq.at[s], sb.at[q], sq_s.at[s], sq_r.at[q], hist + s, c)
+
+    @pl.when(is_hist)
+    def _():
+        @pl.loop(0, hist)
+        def _(k):
+            send_squares(lax.rem(q + k, hist)).start()
+
+    def send_scale(k):
+        return remote(sc, scb.at[q - hist], sc_s.at[k - 1], sc_r.at[k - 1],
+                      hist + lax.rem(q - hist + k, hist), c)
+
+    def send_max(s, k):
+        return remote(mrow.at[s], mb.at[q - hist, s], mx_s.at[s * late + k], mx_r.at[s * late + q - hist], hist + k, c)
+
+    def ratio_out(s):
+        return remote(rt.at[theirs, cols(s)], ratio_ref.at[:, half_col(c, s)], or_s.at[s], or_r.at[s], q, 1 - c)
+
+    def peak_out(s):
+        return remote(hv.at[theirs, cols(s)], peak_ref.at[:, half_col(c, s)], op_s.at[s], op_r.at[s], q, 1 - c)
+
+    @pl.when(is_late)
+    def _():
+        @pl.loop(0, hist)
+        def _(s):
+            remote(sq.at[s], sb.at[s], sq_s.at[s], sq_r.at[s], q - hist, c).wait_recv()
+        give_count.wait_recv()
+        squares = sb[0]
+        for s in range(1, hist):
+            squares = squares + sb[s]
+        count = cnt[...]
+        sigma = jnp.sqrt(squares / (count - COLS) + 1e-06)
+        scale = 1.0 / (sigma * jnp.sqrt(count))
+        sc[...] = scale
+        scb[q - hist] = scale
+
+        @pl.loop(1, hist)
+        def _(k):
+            send_scale(k).start()
+
+        @pl.loop(1, hist)
+        def _(k):
+            send_scale(k).wait_recv()
+
+        for j in range(1, back):
+            send_total(j).wait_recv()
+
+        row = lax.broadcasted_iota(jnp.int32, (chip_rows, chip_rows), 0)
+        col = lax.broadcasted_iota(jnp.int32, (chip_rows, chip_rows), 1)
+        upto = (col <= row).astype(jnp.float32)
+        after = (col > row).astype(jnp.float32)
+        bounds = b_ref[q].astype(jnp.float32) * 0.001
+
+        @pl.loop(0, slots)
+        def _(s):
+            for h in range(2):
+                remote(v_ref.at[:, half_col(h, s)], hv.at[pl.ds(h * rows, rows), cols(s)],
+                       ha_s.at[h * slots + s], ha_r.at[h * slots + s], q, 1 - c).wait_recv()
+            block, offset = word_block(s)
+            flags = clear_bits(hw[:, block], offset, own)
+            early_resid = flags * (hv[:, cols(s)] - dot_high(d_ref[q - back], cb[s]))
+            moving = dot_high(upto, cv[:, cols(s)]) + dot_high(after, early_resid)
+            for j in range(1, back):
+                moving = moving + tt[j - 1, 0:1, cols(s)]
+            ratio = jnp.where(date >= ms_ref[0], moving * scb[s] / bounds, 0.0)
+            rt[:, cols(s)] = ratio
+            best = scan_rows(jnp.abs(ratio), jnp.maximum, 0.0)
+            ccl[:, cols(s)] = best
+            mrow[s] = best[chip_rows - 1 :, :]
+
+            @pl.loop(q - hist + 1, late)
+            def _(k):
+                send_max(s, k).start()
+
+            ratio_out(s).start()
+            ratio_ref[:, half_col(c, s)] = rt[mine, cols(s)]
+
+        @pl.loop(0, slots)
+        def _(s):
+            def earlier(k, best):
+                remote(mrow.at[s], mb.at[k, s], mx_s.at[s * late + k], mx_r.at[s * late + k], q, 1 - c).wait_recv()
+                return jnp.maximum(best, mb[k, s])
+
+            before = lax.fori_loop(0, q - hist, earlier, jnp.zeros((1, own), jnp.float32))
+            hv[:, cols(s)] = jnp.maximum(ccl[:, cols(s)], before)
+            peak_out(s).start()
+            peak_ref[:, half_col(c, s)] = hv[mine, cols(s)]
+
+        @pl.loop(0, slots)
+        def _(s):
+            ratio_out(s).wait()
+            peak_out(s).wait()
+
+            @pl.loop(q - hist + 1, late)
+            def _(k):
+                send_max(s, k).wait_send()
+
+        @pl.loop(1, hist)
+        def _(k):
+            send_scale(k).wait_send()
+            send_coeffs(k, hist).wait_send()
+
+    swap_v.wait_send()
+    swap_w.wait_send()
+
+    @pl.when(is_hist)
+    def _():
+        @pl.loop(1, 2 * hist)
+        def _(k):
+            send_words(k).wait_send()
+
+        @pl.loop(1, hist)
+        def _(k):
+            send_target(k).wait_send()
+            send_coeffs(k, 0).wait_send()
+
+        relay.wait_send()
+        give_count.wait_send()
+
+        @pl.loop(0, hist)
+        def _(s):
+            send_squares(s).wait_send()
+
+    @pl.when(sends_early)
+    def _():
+        for h in range(2):
+            early_words(h).wait_send()
+
+        @pl.loop(0, slots)
+        def _(s):
+            early(0, s).wait_send()
+            early(1, s).wait_send()
+
+    for j in range(1, back):
+        @pl.when(jnp.logical_and(q + j >= hist, q + j < chips))
+        def _():
+            send_total(j).wait_send()
+
+
+def fused_device(narrow, devices, values, cloud_words, history_len, monitor_start, boundary_table):
+    rows, pixels = values.shape
+    chips, chip_rows, half = devices // 2, 2 * rows, pixels // 2
+    dates = boundary_table.shape[0]
+    hist, back = HISTORY_MOST // chip_rows, WINDOW // chip_rows
+    own, late = half // hist, chips - hist
+    design = host_design(dates)
+    lower = [(i, j) for i in range(COLS) for j in range(i + 1)]
+    outer = np.zeros((40, HISTORY_MOST), np.float32)
+    for at, (i, j) in enumerate(lower):
+        outer[at] = design[:HISTORY_MOST, i] * design[:HISTORY_MOST, j]
+    by_chip = design.reshape(chips, chip_rows, COLS)
+    vmem = pl.BlockSpec(memory_space=pltpu.VMEM)
+    smem = pl.BlockSpec(memory_space=pltpu.SMEM)
+    f32, i32, dma = jnp.float32, jnp.int32, pltpu.SemaphoreType.DMA
+    scratch = [
+        pltpu.VMEM((chip_rows, half), f32),
+        pltpu.VMEM((chip_rows, pixels // 32), i32),
+        pltpu.VMEM((chip_rows, half), f32),
+        pltpu.VMEM((chip_rows, half), f32),
+        pltpu.VMEM((chip_rows, pixels // 32), i32),
+        pltpu.VMEM((HISTORY_MOST, 128), i32),
+        pltpu.VMEM((hist, COLS, own), f32),
+        pltpu.VMEM((hist, COLS, own), f32),
+        pltpu.VMEM((40, own), f32),
+        pltpu.VMEM((hist, COLS, own), f32),
+        pltpu.VMEM((1, own), f32),
+        pltpu.VMEM((hist, 1, own), f32),
+        pltpu.VMEM((hist, 1, own), f32),
+        pltpu.VMEM((1, half), f32),
+        pltpu.VMEM((max(back - 1, 1), 1, half), f32),
+        pltpu.VMEM((1, own), f32),
+        pltpu.VMEM((hist, 1, own), f32),
+        pltpu.VMEM((chip_rows, half), f32),
+        pltpu.VMEM((hist, 1, own), f32),
+        pltpu.VMEM((late, hist, 1, own), f32),
+    ]
+    for number in (2, 2 * hist, 2, 2 * hist, hist, hist, 1, hist, max(back - 1, 1), hist, hist * late, hist, hist):
+        scratch += [dma((number,)), dma((number,))]
+    scratch.append(dma((3,)))
+    return pl.pallas_call(
+        functools.partial(fused_kernel, narrow, chips, hist, back),
+        out_shape=[jax.ShapeDtypeStruct((rows, pixels), f32)] * 2,
+        in_specs=[smem, smem] + [vmem] * 6,
+        out_specs=[vmem, vmem],
+        scratch_shapes=scratch,
+        compiler_params=pltpu.CompilerParams(has_side_effects=True, vmem_limit_bytes=40 * 1024 * 1024),
+    )(
+        history_len, monitor_start, values, cloud_words, jnp.asarray(by_chip),
+        jnp.asarray(by_chip.transpose(0, 2, 1)), jnp.asarray(outer),
+        boundary_table.reshape(chips, chip_rows, 1),
+    )
+
+
+def fits(narrow, devices, rows, pixels):
+    chip_rows = 2 * rows
+    if narrow % 2 or rows % 8 or HISTORY_MOST % chip_rows or WINDOW % chip_rows:
+        return False
+    hist = HISTORY_MOST // chip_rows
+    return devices // 2 == 2 * hist and (pixels // 2) % (hist * 128) == 0 and 128 % (pixels // 64 // hist) == 0
+
+
 def solution(mesh):
+    narrow = mesh.shape["narrow"]
+    devices = narrow * mesh.shape["wide"]
+
+    def per_device_any(values, *rest):
+        if fits(narrow, devices, *values.shape):
+            return fused_device(narrow, devices, values, *rest)
+        return per_device(values, *rest)
+
     placed = (P(("wide", "narrow"), None), P(("wide", "narrow"), None), P(), P(), P())
     return jax.shard_map(
-        per_device,
+        per_device_any,
         mesh=mesh,
         in_specs=placed,
         out_specs=(P(("wide", "narrow"), None), P(("wide", "narrow"), None)),

time: 93.1 us -> 67.8 us (0.73)
  the two profiles are of different devices: /device:TPU:0 before, /device:TPU:25 now
where the time goes in v2:
time: 67.8 us; the launch traced here: 67.4 us
  Pallas kernels  59 us (87%)
  local copies, waits for them, and re-layouts  6.43 us (9%)
  between operations  2.01 us (3%)
    pallas_call x1, Pallas kernels, fused_device(): pl.pallas_call(functools.partial(fused_kernel, narrow, chips, hist, back)...  59 us
    unnamed x12, local copies, waits for them, and re-layouts  5.54 us

profile of v2, /device:TPU:25, one launch (start us, length us, event | category | flops | bytes accessed | tf_op | source)
XLA Modules:
  0.0 67.4 jit_solution(2407180647405367497)
XLA Ops:
  0.6 0.0 copy-start.1
  2.0 0.9 %reshape.8.b_ref = s32[16,32,1]{2,1,0:T(8,128)S(1)} reshape(s32[512]{0:T(512)} %param.12) | data formatting | bytes 4096 | tf_op jit(solution)/shard_map/reshape | solution.py:562
  2.9 0.0 copy-done.1
  2.9 0.0 copy-start
  2.9 1.2 %copy-done = f32[16,16384]{1,0:T(8,128)S(1)} copy-done((f32[16,16384]{1,0:T(8,128)S(1)}, f32[16,16384]{1,0:T(8,128)}, u32[]{:S(2)}) %copy-start) | copy-done | bytes 1048600
  4.1 0.0 copy-start.2
  4.1 0.8 %copy-done.2 = f32[16,8,32]{2,1,0:T(8,128)S(1)} copy-done((f32[16,8,32]{2,1,0:T(8,128)S(1)}, f32[16,8,32]{2,1,0:T(8,128)}, u32[]{:S(2)}) %copy-start.2) | copy-done | bytes 16408
  4.9 0.0 copy-start.3
  5.0 0.8 %copy-done.3 = f32[40,256]{1,0:T(8,128)S(1)} copy-done((f32[40,256]{1,0:T(8,128)S(1)}, f32[40,256]{1,0:T(8,128)}, u32[]{:S(2)}) %copy-start.3) | copy-done | bytes 40984
  5.7 0.0 copy-start.4
  5.7 0.8 %copy-done.4 = s32[16,512]{1,0:T(8,128)S(1)} copy-done((s32[16,512]{1,0:T(8,128)S(1)}, s32[16,512]{1,0:T(8,128)}, u32[]{:S(2)}) %copy-start.4) | copy-done | bytes 32792
  6.5 59.0 %shard_map.95 = (f32[16,16384]{1,0:T(8,128)S(1)}, f32[16,16384]{1,0:T(8,128)S(1)}) custom-call(s32[1]{0:T(128)S(6)} %copy.13.hl_ref, s32[1]{0:T(128)S(6)} %copy.14.ms_ref, f32[16,16384]{1,0:T(8,128)S(1)} %copy-done, s32[16,512]{1,0:T(8,128)S(1)} %copy-done.4, f32[16,32,8]{2,1,0:T(8,128)S(1)} %copy-done.1, f32[16,8,32]{2,1,0:T(8,128)S(1)} %copy-done.2, ...), custom_call_target="tpu_custom_call" | custom-call | tf_op jit(solution)/shard_map/pallas_call | solution.py:552
  65.5 1.0 %copy.15 = f32[16,16384]{1,0:T(8,128)} copy(f32[16,16384]{1,0:T(8,128)S(1)} %get-tuple-element.4) | data formatting | bytes 2097152
  66.4 1.0 %copy.16 = f32[16,16384]{1,0:T(8,128)} copy(f32[16,16384]{1,0:T(8,128)S(1)} %get-tuple-element.5) | data formatting | bytes 2097152
Async XLA Ops:
  0.6 2.2 %copy-start.1 = (f32[16,32,8]{2,1,0:T(8,128)S(1)}, f32[16,32,8]{2,1,0:T(8,128)}, u32[]{:S(2)}) copy-start(f32[16,32,8]{2,1,0:T(8,128)} %constant.6.clone.d_ref) | copy-start | bytes 49156
  2.9 1.2 %copy-start = (f32[16,16384]{1,0:T(8,128)S(1)}, f32[16,16384]{1,0:T(8,128)}, u32[]{:S(2)}) copy-start(f32[16,16384]{1,0:T(8,128)} %v_ref.1) | copy-start | bytes 3145732
  4.1 0.8 %copy-start.2 = (f32[16,8,32]{2,1,0:T(8,128)S(1)}, f32[16,8,32]{2,1,0:T(8,128)}, u32[]{:S(2)}) copy-start(f32[16,8,32]{2,1,0:T(8,128)} %constant.7.clone.dt_ref) | copy-start | bytes 49156
  4.9 0.8 %copy-start.3 = (f32[40,256]{1,0:T(8,128)S(1)}, f32[40,256]{1,0:T(8,128)}, u32[]{:S(2)}) copy-start(f32[40,256]{1,0:T(8,128)} %constant.8.clone.ot_ref) | copy-start | bytes 122884
  5.7 0.8 %copy-start.4 = (s32[16,512]{1,0:T(8,128)S(1)}, s32[16,512]{1,0:T(8,128)}, u32[]{:S(2)}) copy-start(s32[16,512]{1,0:T(8,128)} %w_ref.1) | copy-start | bytes 98308

commit v3 on v2

--- a/solution.py
+++ b/solution.py
@@ -136,14 +136,23 @@
 
 
 def scan_rows(array, combine, neutral):
-    rows = array.shape[0]
-    row = lax.broadcasted_iota(jnp.int32, array.shape, 0)
-    step = 1
-    while step < rows:
-        shifted = jnp.where(row >= step, pltpu.roll(array, step, 0), neutral)
-        array = combine(array, shifted)
-        step *= 2
-    return array
+    tiles = []
+    row = lax.broadcasted_iota(jnp.int32, (8, array.shape[1]), 0)
+    for at in range(0, array.shape[0], 8):
+        tile = array[at : at + 8]
+        for step in (1, 2, 4):
+            tile = combine(tile, jnp.where(row >= step, pltpu.roll(tile, step, 0), neutral))
+        if tiles:
+            tile = combine(tile, tiles[-1][7:8])
+        tiles.append(tile)
+    return jnp.concatenate(tiles, axis=0)
+
+
+def fitted(design, coeffs):
+    total = design[:, 0:1] * coeffs[0:1]
+    for k in range(1, COLS):
+        total = total + design[:, k : k + 1] * coeffs[k : k + 1]
+    return total
 
 
 def solve_rows(entry, target):
@@ -175,8 +184,8 @@
 
 def fused_kernel(
     narrow, chips, hist, back,
-    hl_ref, ms_ref, v_ref, w_ref, d_ref, dt_ref, ot_ref, b_ref, ratio_ref, peak_ref,
-    cv, cw, ccl, hv, hw, ow, tp, tb, nm, cb, cnt, sq, sb, tot, tt, sc, scb, rt, mrow, mb,
+    hl_ref, ms_ref, b_ref, v_ref, w_ref, d_hbm, ot_hbm, ratio_ref, peak_ref,
+    cv, cw, ccl, hv, hw, ow, tp, tb, nm, cb, cnt, sq, sb, tot, tt, sc, scb, rt, mrow, mb, rin, pin, dm, de, ot_ref,
     ax_s, ax_r, ha_s, ha_r, hw_s, hw_r, ow_s, ow_r, tp_s, tp_r, cb_s, cb_r, ct_s, ct_r,
     sq_s, sq_r, tt_s, tt_r, sc_s, sc_r, mx_s, mx_r, or_s, or_r, op_s, op_r, lc,
 ):
@@ -215,6 +224,12 @@
     swap_w = remote(w_ref, cw.at[mine, :], ax_s.at[1], ax_r.at[1], q, 1 - c)
     swap_w.start()
     swap_v.start()
+    get_d = pltpu.make_async_copy(d_hbm.at[q], dm, lc.at[3])
+    get_e = pltpu.make_async_copy(d_hbm.at[lax.max(q - back, 0)], de, lc.at[4])
+    get_o = pltpu.make_async_copy(ot_hbm, ot_ref, lc.at[5])
+    get_d.start()
+    get_e.start()
+    get_o.start()
     keep_v = pltpu.make_async_copy(v_ref.at[:, my_half], cv.at[mine, :], lc.at[0])
     keep_w = pltpu.make_async_copy(w_ref, cw.at[mine, :], lc.at[1])
     keep_v.start()
@@ -248,15 +263,26 @@
         return remote(v_ref.at[:, half_col(h, s)], hv.at[mine, cols(s)],
                       ha_s.at[h * slots + s], ha_r.at[c * slots + s], q + back, h)
 
+    third, most = slots // 4, slots * 5 // 8
+
+    def start_early(low, high):
+        @pl.when(sends_early)
+        def _():
+            @pl.loop(low, high)
+            def _(s):
+                early(0, s).start()
+                early(1, s).start()
+
     @pl.when(sends_early)
     def _():
         for h in range(2):
             early_words(h).start()
 
-        @pl.loop(0, slots)
-        def _(s):
-            early(0, s).start()
-            early(1, s).start()
+    start_early(0, third)
+
+    @pl.when(is_late)
+    def _():
+        start_early(third, most)
 
     def word_block(s):
         start = c * (half // 32) + s * (own // 32)
@@ -273,6 +299,9 @@
 
     keep_v.wait()
     swap_v.wait_recv()
+    get_d.wait()
+    get_e.wait()
+    get_o.wait()
     date = q * chip_rows + lax.broadcasted_iota(jnp.int32, (chip_rows, own), 0)
 
     def send_target(k):
@@ -291,12 +320,14 @@
         @pl.loop(0, slots)
         def _(s):
             weighted = jnp.where(date < hl_ref[0], ccl[:, cols(s)] * cv[:, cols(s)], 0.0)
-            tp[s] = dot_high(dt_ref[q], weighted)
+            for k in range(COLS):
+                tp[s, k : k + 1, :] = jnp.sum(weighted * dm[:, k : k + 1], axis=0, keepdims=True)
 
         @pl.loop(1, hist)
         def _(k):
             send_target(k).start()
 
+        start_early(third, most)
         ratio_ref[...] = jnp.zeros_like(ratio_ref)
         peak_ref[...] = jnp.zeros_like(peak_ref)
         keep_o.wait()
@@ -336,6 +367,8 @@
         def _(k):
             send_coeffs(k, 0).start()
 
+        start_early(most, slots)
+
         @pl.loop(1, hist)
         def _(k):
             send_coeffs(k, 0).wait_recv()
@@ -344,11 +377,19 @@
     def _():
         for h in range(2):
             remote(w_ref, hw.at[pl.ds(h * rows, rows), :], hw_s.at[h], hw_r.at[h], q, 1 - c).wait_recv()
+
+        @pl.loop(0, slots)
+        def _(s):
+            block, offset = word_block(s)
+            rt[:, cols(s)] = clear_bits(hw[:, block], offset, own)
+
         remote(cb.at[q - hist], cb.at[q - hist], cb_s.at[hist - 1], cb_r.at[hist - 1], q - hist, c).wait_recv()
 
         @pl.loop(1, hist)
         def _(k):
             send_coeffs(k, hist).start()
+
+        start_early(most, slots)
 
         @pl.loop(1, hist)
         def _(k):
@@ -356,7 +397,7 @@
 
     @pl.loop(0, slots)
     def _(s):
-        resid = ccl[:, cols(s)] * (cv[:, cols(s)] - dot_high(d_ref[q], cb[s]))
+        resid = ccl[:, cols(s)] * (cv[:, cols(s)] - fitted(dm[...], cb[s]))
         cv[:, cols(s)] = resid
         tot[0:1, cols(s)] = jnp.sum(resid, axis=0, keepdims=True)
         sq[s] = jnp.sum(jnp.where(date < hl_ref[0], resid * resid, 0.0), axis=0, keepdims=True)
@@ -379,20 +420,56 @@
             send_squares(lax.rem(q + k, hist)).start()
 
     def send_scale(k):
-        return remote(sc, scb.at[q - hist], sc_s.at[k - 1], sc_r.at[k - 1],
-                      hist + lax.rem(q - hist + k, hist), c)
+        to = lax.rem(me - 2 * hist + k, 2 * late)
+        return remote(sc, scb.at[c, q - hist], sc_s.at[k - 1], sc_r.at[k - 1],
+                      hist + lax.div(to, 2), lax.rem(to, 2))
 
     def send_max(s, k):
         return remote(mrow.at[s], mb.at[q - hist, s], mx_s.at[s * late + k], mx_r.at[s * late + q - hist], hist + k, c)
 
     def ratio_out(s):
-        return remote(rt.at[theirs, cols(s)], ratio_ref.at[:, half_col(c, s)], or_s.at[s], or_r.at[s], q, 1 - c)
+        return remote(rt.at[theirs, cols(s)], rin.at[:, cols(s)], or_s.at[s], or_r.at[s], q, 1 - c)
 
     def peak_out(s):
-        return remote(hv.at[theirs, cols(s)], peak_ref.at[:, half_col(c, s)], op_s.at[s], op_r.at[s], q, 1 - c)
+        return remote(hv.at[theirs, cols(s)], pin.at[:, cols(s)], op_s.at[s], op_r.at[s], q, 1 - c)
 
     @pl.when(is_late)
     def _():
+        row = lax.broadcasted_iota(jnp.int32, (chip_rows, 128), 0)
+        bounds = jnp.zeros((chip_rows, 128), jnp.int32)
+        for i in range(chip_rows):
+            bounds = jnp.where(row == i, b_ref[q * chip_rows + i], bounds)
+        over = 1.0 / (bounds[:, 0:1].astype(jnp.float32) * 0.001)
+
+        @pl.loop(0, slots)
+        def _(s):
+            for h in range(2):
+                remote(v_ref.at[:, half_col(h, s)], hv.at[pl.ds(h * rows, rows), cols(s)],
+                       ha_s.at[h * slots + s], ha_r.at[h * slots + s], q, 1 - c).wait_recv()
+            early_resid = rt[:, cols(s)] * (hv[:, cols(s)] - fitted(de[...], cb[s]))
+            change = cv[:, cols(s)] - early_resid
+            rt[:, cols(s)] = scan_rows(change, jnp.add, 0.0) + jnp.sum(early_resid, axis=0, keepdims=True)
+
+        for j in range(1, back):
+            send_total(j).wait_recv()
+
+        @pl.loop(0, slots)
+        def _(s):
+            moving = rt[:, cols(s)]
+            for j in range(1, back):
+                moving = moving + tt[j - 1, 0:1, cols(s)]
+            ratio = jnp.where(date >= ms_ref[0], moving * over, 0.0)
+            rt[:, cols(s)] = ratio
+            best = scan_rows(jnp.abs(ratio), jnp.maximum, 0.0)
+            ccl[:, cols(s)] = best
+            mrow[s] = best[chip_rows - 1 :, :]
+
+            @pl.loop(q - hist + 1, late)
+            def _(k):
+                send_max(s, k).start()
+
+            ratio_out(s).start()
+
         @pl.loop(0, hist)
         def _(s):
             remote(sq.at[s], sb.at[s], sq_s.at[s], sq_r.at[s], q - hist, c).wait_recv()
@@ -404,48 +481,11 @@
         sigma = jnp.sqrt(squares / (count - COLS) + 1e-06)
         scale = 1.0 / (sigma * jnp.sqrt(count))
         sc[...] = scale
-        scb[q - hist] = scale
-
-        @pl.loop(1, hist)
+        scb[c, q - hist] = scale
+
+        @pl.loop(1, 2 * late)
         def _(k):
             send_scale(k).start()
-
-        @pl.loop(1, hist)
-        def _(k):
-            send_scale(k).wait_recv()
-
-        for j in range(1, back):
-            send_total(j).wait_recv()
-
-        row = lax.broadcasted_iota(jnp.int32, (chip_rows, chip_rows), 0)
-        col = lax.broadcasted_iota(jnp.int32, (chip_rows, chip_rows), 1)
-        upto = (col <= row).astype(jnp.float32)
-        after = (col > row).astype(jnp.float32)
-        bounds = b_ref[q].astype(jnp.float32) * 0.001
-
-        @pl.loop(0, slots)
-        def _(s):
-            for h in range(2):
-                remote(v_ref.at[:, half_col(h, s)], hv.at[pl.ds(h * rows, rows), cols(s)],
-                       ha_s.at[h * slots + s], ha_r.at[h * slots + s], q, 1 - c).wait_recv()
-            block, offset = word_block(s)
-            flags = clear_bits(hw[:, block], offset, own)
-            early_resid = flags * (hv[:, cols(s)] - dot_high(d_ref[q - back], cb[s]))
-            moving = dot_high(upto, cv[:, cols(s)]) + dot_high(after, early_resid)
-            for j in range(1, back):
-                moving = moving + tt[j - 1, 0:1, cols(s)]
-            ratio = jnp.where(date >= ms_ref[0], moving * scb[s] / bounds, 0.0)
-            rt[:, cols(s)] = ratio
-            best = scan_rows(jnp.abs(ratio), jnp.maximum, 0.0)
-            ccl[:, cols(s)] = best
-            mrow[s] = best[chip_rows - 1 :, :]
-
-            @pl.loop(q - hist + 1, late)
-            def _(k):
-                send_max(s, k).start()
-
-            ratio_out(s).start()
-            ratio_ref[:, half_col(c, s)] = rt[mine, cols(s)]
 
         @pl.loop(0, slots)
         def _(s):
@@ -456,20 +496,40 @@
             before = lax.fori_loop(0, q - hist, earlier, jnp.zeros((1, own), jnp.float32))
             hv[:, cols(s)] = jnp.maximum(ccl[:, cols(s)], before)
             peak_out(s).start()
-            peak_ref[:, half_col(c, s)] = hv[mine, cols(s)]
-
-        @pl.loop(0, slots)
-        def _(s):
-            ratio_out(s).wait()
-            peak_out(s).wait()
+
+        @pl.loop(1, 2 * late)
+        def _(k):
+            send_scale(k).wait_recv()
+
+        @pl.loop(0, slots)
+        def _(s):
+            scale = scb[c, s]
+            ratio_ref[:, half_col(c, s)] = rt[mine, cols(s)] * scale
+            peak_ref[:, half_col(c, s)] = hv[mine, cols(s)] * scale
+
+        @pl.loop(0, slots)
+        def _(s):
+            ratio_out(s).wait_recv()
+            peak_out(s).wait_recv()
+            scale = scb[1 - c, s]
+            ratio_ref[:, half_col(1 - c, s)] = rin[:, cols(s)] * scale
+            peak_ref[:, half_col(1 - c, s)] = pin[:, cols(s)] * scale
+
+        @pl.loop(0, slots)
+        def _(s):
+            ratio_out(s).wait_send()
+            peak_out(s).wait_send()
 
             @pl.loop(q - hist + 1, late)
             def _(k):
                 send_max(s, k).wait_send()
 
-        @pl.loop(1, hist)
+        @pl.loop(1, 2 * late)
         def _(k):
             send_scale(k).wait_send()
+
+        @pl.loop(1, hist)
+        def _(k):
             send_coeffs(k, hist).wait_send()
 
     swap_v.wait_send()
@@ -522,6 +582,7 @@
         outer[at] = design[:HISTORY_MOST, i] * design[:HISTORY_MOST, j]
     by_chip = design.reshape(chips, chip_rows, COLS)
     vmem = pl.BlockSpec(memory_space=pltpu.VMEM)
+    hbm = pl.BlockSpec(memory_space=pl.ANY)
     smem = pl.BlockSpec(memory_space=pltpu.SMEM)
     f32, i32, dma = jnp.float32, jnp.int32, pltpu.SemaphoreType.DMA
     scratch = [
@@ -541,25 +602,29 @@
         pltpu.VMEM((1, half), f32),
         pltpu.VMEM((max(back - 1, 1), 1, half), f32),
         pltpu.VMEM((1, own), f32),
-        pltpu.VMEM((hist, 1, own), f32),
+        pltpu.VMEM((2, late, 1, own), f32),
         pltpu.VMEM((chip_rows, half), f32),
         pltpu.VMEM((hist, 1, own), f32),
         pltpu.VMEM((late, hist, 1, own), f32),
+        pltpu.VMEM((rows, half), f32),
+        pltpu.VMEM((rows, half), f32),
+        pltpu.VMEM((chip_rows, COLS), f32),
+        pltpu.VMEM((chip_rows, COLS), f32),
+        pltpu.VMEM((40, HISTORY_MOST), f32),
     ]
-    for number in (2, 2 * hist, 2, 2 * hist, hist, hist, 1, hist, max(back - 1, 1), hist, hist * late, hist, hist):
+    for number in (2, 2 * hist, 2, 2 * hist, hist, hist, 1, hist, max(back - 1, 1), 2 * late, hist * late, hist, hist):
         scratch += [dma((number,)), dma((number,))]
-    scratch.append(dma((3,)))
+    scratch.append(dma((6,)))
     return pl.pallas_call(
         functools.partial(fused_kernel, narrow, chips, hist, back),
         out_shape=[jax.ShapeDtypeStruct((rows, pixels), f32)] * 2,
-        in_specs=[smem, smem] + [vmem] * 6,
+        in_specs=[smem, smem, smem, vmem, vmem, hbm, hbm],
         out_specs=[vmem, vmem],
         scratch_shapes=scratch,
         compiler_params=pltpu.CompilerParams(has_side_effects=True, vmem_limit_bytes=40 * 1024 * 1024),
     )(
-        history_len, monitor_start, values, cloud_words, jnp.asarray(by_chip),
-        jnp.asarray(by_chip.transpose(0, 2, 1)), jnp.asarray(outer),
-        boundary_table.reshape(chips, chip_rows, 1),
+        history_len, monitor_start, boundary_table, values, cloud_words,
+        jnp.asarray(by_chip), jnp.asarray(outer),
     )
 
 

time: 67.8 us -> 60.6 us (0.89)
  the two profiles are of different devices: /device:TPU:25 before, /device:TPU:17 now
where the time goes in v3:
time: 60.6 us; the launch traced here: 60.2 us
  Pallas kernels  52.6 us (87%)
  local copies, waits for them, and re-layouts  5.65 us (9%)
  between operations  1.97 us (3%)
    pallas_call x1, Pallas kernels, fused_device(): pl.pallas_call(functools.partial(fused_kernel, narrow, chips, hist, back)...  52.6 us
    unnamed x12, local copies, waits for them, and re-layouts  5.65 us

profile of v3, /device:TPU:17, one launch (start us, length us, event | category | flops | bytes accessed | tf_op | source)
XLA Modules:
  0.0 60.2 jit_solution(12415816255656437635)
XLA Ops:
  0.6 0.0 copy-start.4
  1.9 0.0 copy-done.4
  2.0 0.0 copy-start
  2.0 1.2 %copy-done = f32[16,16384]{1,0:T(8,128)S(1)} copy-done((f32[16,16384]{1,0:T(8,128)S(1)}, f32[16,16384]{1,0:T(8,128)}, u32[]{:S(2)}) %copy-start) | copy-done | bytes 1048600
  3.2 0.0 copy-start.1
  3.2 0.9 %copy-done.1 = f32[16,32,8]{2,1,0:T(8,128)S(1)} copy-done((f32[16,32,8]{2,1,0:T(8,128)S(1)}, f32[16,32,8]{2,1,0:T(8,128)}, u32[]{:S(2)}) %copy-start.1) | copy-done | bytes 16408
  4.1 0.0 copy-start.2
  4.1 0.8 %copy-done.2 = f32[40,256]{1,0:T(8,128)S(1)} copy-done((f32[40,256]{1,0:T(8,128)S(1)}, f32[40,256]{1,0:T(8,128)}, u32[]{:S(2)}) %copy-start.2) | copy-done | bytes 40984
  4.9 0.0 copy-start.3
  4.9 0.8 %copy-done.3 = s32[16,512]{1,0:T(8,128)S(1)} copy-done((s32[16,512]{1,0:T(8,128)S(1)}, s32[16,512]{1,0:T(8,128)}, u32[]{:S(2)}) %copy-start.3) | copy-done | bytes 32792
  5.7 52.6 %shard_map.86 = (f32[16,16384]{1,0:T(8,128)S(1)}, f32[16,16384]{1,0:T(8,128)S(1)}) custom-call(s32[1]{0:T(128)S(6)} %copy.11.hl_ref, s32[1]{0:T(128)S(6)} %copy.12.ms_ref, s32[512]{0:T(512)S(1)} %copy-done.4, f32[16,16384]{1,0:T(8,128)S(1)} %copy-done, s32[16,512]{1,0:T(8,128)S(1)} %copy-done.3, f32[16,32,8]{2,1,0:T(8,128)S(1)} %copy-done.1, ...), custom_call_target="tpu_custom_call" | custom-call | tf_op jit(solution)/shard_map/pallas_call | solution.py:618
  58.3 1.0 %copy.13 = f32[16,16384]{1,0:T(8,128)} copy(f32[16,16384]{1,0:T(8,128)S(1)} %get-tuple-element.4) | data formatting | bytes 2097152
  59.2 1.0 %copy.14 = f32[16,16384]{1,0:T(8,128)} copy(f32[16,16384]{1,0:T(8,128)S(1)} %get-tuple-element.5) | data formatting | bytes 2097152
Async XLA Ops:
  0.6 1.3 %copy-start.4 = (s32[512]{0:T(512)S(1)}, s32[512]{0:T(512)}, u32[]{:S(2)}) copy-start(s32[512]{0:T(512)} %b_ref.1) | copy-start | bytes 6148
  2.0 1.2 %copy-start = (f32[16,16384]{1,0:T(8,128)S(1)}, f32[16,16384]{1,0:T(8,128)}, u32[]{:S(2)}) copy-start(f32[16,16384]{1,0:T(8,128)} %v_ref.1) | copy-start | bytes 3145732
  3.2 0.9 %copy-start.1 = (f32[16,32,8]{2,1,0:T(8,128)S(1)}, f32[16,32,8]{2,1,0:T(8,128)}, u32[]{:S(2)}) copy-start(f32[16,32,8]{2,1,0:T(8,128)} %constant.4.clone.d_hbm) | copy-start | bytes 49156
  4.1 0.8 %copy-start.2 = (f32[40,256]{1,0:T(8,128)S(1)}, f32[40,256]{1,0:T(8,128)}, u32[]{:S(2)}) copy-start(f32[40,256]{1,0:T(8,128)} %constant.5.clone.ot_hbm) | copy-start | bytes 122884
  4.9 0.8 %copy-start.3 = (s32[16,512]{1,0:T(8,128)S(1)}, s32[16,512]{1,0:T(8,128)}, u32[]{:S(2)}) copy-start(s32[16,512]{1,0:T(8,128)} %w_ref.1) | copy-start | bytes 98308

commit v4 on v3

--- a/solution.py
+++ b/solution.py
@@ -621,7 +621,7 @@
         in_specs=[smem, smem, smem, vmem, vmem, hbm, hbm],
         out_specs=[vmem, vmem],
         scratch_shapes=scratch,
-        compiler_params=pltpu.CompilerParams(has_side_effects=True, vmem_limit_bytes=40 * 1024 * 1024),
+        compiler_params=pltpu.CompilerParams(has_side_effects=True),
     )(
         history_len, monitor_start, boundary_table, values, cloud_words,
         jnp.asarray(by_chip), jnp.asarray(outer),

time: 60.6 us -> 60.4 us (level)
  Pallas kernels: 52.6 us -> 55 us
  local copies, waits for them, and re-layouts: 5.65 us -> 3.32 us
    pallas_call x1, Pallas kernels: 52.6 us -> 55 us  [fused_device(): pl.pallas_call(functools.partial(fused_kernel, narrow, chips, hist, back)...]
    unnamed x12 -> x4, local copies, waits for them, and re-layouts: 5.65 us -> 3.32 us
where the time goes in v4:
time: 60.4 us; the launch traced here: 60.2 us
  Pallas kernels  55 us (91%)
  local copies, waits for them, and re-layouts  3.32 us (5%)
  between operations  1.94 us (3%)
    pallas_call x1, Pallas kernels, fused_device(): pl.pallas_call(functools.partial(fused_kernel, narrow, chips, hist, back)...  55 us
    unnamed x4, local copies, waits for them, and re-layouts  3.32 us

profile of v4, /device:TPU:17, one launch (start us, length us, event | category | flops | bytes accessed | tf_op | source)
XLA Modules:
  0.0 60.2 jit_solution(1690836045393875904)
XLA Ops:
  1.9 55.0 %shard_map.86 = (f32[16,16384]{1,0:T(8,128)}, f32[16,16384]{1,0:T(8,128)}) custom-call(s32[1]{0:T(128)S(6)} %copy.11.hl_ref, s32[1]{0:T(128)S(6)} %copy.12.ms_ref, s32[512]{0:T(512)} %b_ref.1, f32[16,16384]{1,0:T(8,128)} %v_ref.1, s32[16,512]{1,0:T(8,128)} %w_ref.1, f32[16,32,8]{2,1,0:T(8,128)} %constant.4.clone.d_hbm, f32[40,256]{1,0:T(8,128)} %constant.5.clone.ot_hbm), custom_call_target="tpu_custom_call" | custom-call | tf_op jit(solution)/shard_map/pallas_call | solution.py:618
  56.9 0.0 copy-start
  56.9 2.4 %copy.13 = f32[16,16384]{1,0:T(8,128)} copy(f32[16,16384]{1,0:T(8,128)} %get-tuple-element.4) | data formatting | bytes 2097152
  59.3 0.0 copy-done
  59.3 1.0 %copy.14 = f32[16,16384]{1,0:T(8,128)} copy(f32[16,16384]{1,0:T(8,128)S(1)} %copy-done) | data formatting | bytes 2097152
Async XLA Ops:
  56.9 2.4 %copy-start = (f32[16,16384]{1,0:T(8,128)S(1)}, f32[16,16384]{1,0:T(8,128)}, u32[]{:S(2)}) copy-start(f32[16,16384]{1,0:T(8,128)} %get-tuple-element.5) | copy-start | bytes 3145732
